TPU v7x, 32 devices: a whole 2x2x4 slice. The times are simulated.
32 devices in a mesh: gz: 8 (over z, x), gy: 4 (over y, core).
Axes of the slice: x: 2, y: 2, z: 4, core: 2. Of those that a mesh axis runs over, the one named last changes fastest.
Arguments:
- source_first: float32 [64, 32, 16, 128], P('gz', 'gy'), may hold values from -6 to 6
- source_second: float32 [32, 16, 16, 128], P('gz', 'gy'), may hold values from -6 to 6
- source_third: float32 [16, 8, 16, 128], P('gz', 'gy'), may hold values from -6 to 6
- source_fourth: float32 [8, 4, 16, 128], P('gz', 'gy'), may hold values from -6 to 6
- guess_first: float32 [64, 32, 16, 128], P('gz', 'gy'), may hold values from -6 to 6
- guess_second: float32 [32, 16, 16, 128], P('gz', 'gy'), may hold values from -6 to 6
- guess_third: float32 [16, 8, 16, 128], P('gz', 'gy'), may hold values from -6 to 6
- guess_fourth: float32 [8, 4, 16, 128], P('gz', 'gy'), may hold values from -6 to 6
- shift_first: float32 [64, 32, 128], P('gz', 'gy'), may hold values from 0.2 to 2
- shift_second: float32 [32, 16, 128], P('gz', 'gy'), may hold values from 0.2 to 2
- shift_third: float32 [16, 8, 128], P('gz', 'gy'), may hold values from 0.2 to 2
- shift_fourth: float32 [8, 4, 128], P('gz', 'gy'), may hold values from 0.2 to 2
- blocks_first: bfloat16 [64, 32, 2, 128, 128], P('gz', 'gy'), may hold values from -0.375 to 0.375
- blocks_second: bfloat16 [32, 16, 2, 128, 128], P('gz', 'gy'), may hold values from -0.375 to 0.375
- blocks_third: bfloat16 [16, 8, 2, 128, 128], P('gz', 'gy'), may hold values from -0.375 to 0.375
- links_first: int32 [64, 32, 2], P('gz', 'gy'), may hold values from 0 to 511, as said below
- links_second: int32 [32, 16, 2], P('gz', 'gy'), may hold values from 0 to 127, as said below
- links_third: int32 [16, 8, 2], P('gz', 'gy'), may hold values from 0 to 31, as said below
Outputs:
- smooth_first: float32 [64, 32, 16, 128], P('gz', 'gy')
- smooth_second: float32 [32, 16, 16, 128], P('gz', 'gy')
- smooth_third: float32 [16, 8, 16, 128], P('gz', 'gy')
- smooth_fourth: float32 [8, 4, 16, 128], P('gz', 'gy')
Inputs may be any that keep to these rules, and one draw needn't show every extreme that they name: `links_first`: entry k of fine cell (i, j) names coarse column x * 16 + y with x within one of i // 2 and y within one of j // 2, both periodic on the coarse grid. `links_second`: entry k of cell (i, j) names coarse column x * 8 + y with x within one of i // 2 and y within one of j // 2, both periodic on the coarse grid. `links_third`: entry k of cell (i, j) names coarse column x * 4 + y with x within one of i // 2 and y within one of j // 2, both periodic on the coarse grid.
All inputs are finite; a program needn't handle non-finite values.
Results may differ from a plain program's by a relative error of at most 0.0005.
Values may be sent and summed in bfloat16 or wider, within the bound.
A program may use at most 256 MiB of HBM per device.

v0:
```python
from functools import partial

import jax
import jax.numpy as jnp
from jax import lax
from jax.experimental import pallas as pl
from jax.experimental.pallas import tpu as pltpu
from jax.sharding import PartitionSpec as P

DEGREE = 3
LEVELS = 4
REACH = DEGREE

upper_edge = 14.0
lower_edge = upper_edge / 8.0


def coefficients():
    centre = (upper_edge + lower_edge) / 2.0
    half_width = (upper_edge - lower_edge) / 2.0
    ratio = centre / half_width
    factor = 1.0 / ratio
    steps = []
    for _ in range(DEGREE - 1):
        following = 1.0 / (2.0 * ratio - factor)
        steps.append((following * factor, 2.0 * following / half_width))
        factor = following
    return 1.0 / centre, steps


def span(offset, length, reach):
    low = max(offset * length, -reach)
    high = min((offset + 1) * length, length + reach)
    return low, high


def plan(nx, ny, reach, box):
    out = []
    far_x, far_y = -(-reach // nx), -(-reach // ny)
    for ox in range(-far_x, far_x + 1):
        for oy in range(-far_y, far_y + 1):
            if ox == 0 and oy == 0:
                continue
            limit = reach - 1 if (ox and oy and not box) else reach
            rows, cols = span(-ox, nx, limit), span(-oy, ny, limit)
            if rows[0] >= rows[1] or cols[0] >= cols[1]:
                continue
            far = (nx * (abs(ox) - 1) + 1 if ox else 0) + (ny * (abs(oy) - 1) + 1 if oy else 0)
            if not box and far > reach:
                continue
            source = (rows[0] + ox * nx, cols[0] + oy * ny)
            out.append((ox, oy, source, (rows[0], cols[0]), (rows[1] - rows[0], cols[1] - cols[0])))
    out.sort(key=lambda m: (abs(m[0]) + abs(m[1]), m))
    return out


def modulo(value, size):
    if size & (size - 1) == 0:
        return jnp.bitwise_and(value, size - 1)
    return lax.rem(value, size)


def quotient(value, size):
    if size & (size - 1) == 0:
        return jnp.right_shift(value, size.bit_length() - 1)
    return lax.div(value, size)


class Counter:
    def __init__(self):
        self.used = 0

    def take(self):
        self.used += 1
        return self.used - 1


def message_count(dims):
    total = 0
    for level, (nx, ny) in enumerate(dims):
        total += len(plan(nx, ny, REACH, False)) + 2 * len(plan(nx, ny, REACH - 1, False))
        if level:
            total += len(plan(nx, ny, 1, True))
    return total


def partners(dims, peers):
    found = set()
    for level, (nx, ny) in enumerate(dims):
        for m in plan(nx, ny, REACH, False) + plan(nx, ny, 1, True):
            found.add((m[0] % peers[0], m[1] % peers[1]))
            found.add((-m[0] % peers[0], -m[1] % peers[1]))
    return sorted(found)


def kernel(dims, peers, *refs):
    sources, guesses, shifts = refs[0:4], refs[4:8], refs[8:12]
    blocks, links = refs[12:15], refs[15:18]
    outs = refs[18:22]
    U, S, D, R, P0, P1, O = (refs[22 + 4 * k : 26 + 4 * k] for k in range(7))
    B, C, H = refs[50:53], refs[53:56], refs[56:60]
    local_sem, send_sem, recv_sem = refs[60:63]
    gz, gy = lax.axis_index("gz"), lax.axis_index("gy")

    def at(ox, oy):
        return (lax.rem(gz + (ox % peers[0]), peers[0]), lax.rem(gy + (oy % peers[1]), peers[1]))

    barrier = pltpu.get_barrier_semaphore()
    company = partners(dims, peers)
    for ox, oy in company:
        pl.semaphore_signal(barrier, inc=1, device_id=at(ox, oy), device_id_type=pl.DeviceIdType.MESH)

    local = Counter()

    def fetch(source, target):
        copy = pltpu.make_async_copy(source, target, local_sem.at[local.take()])
        copy.start()
        return copy

    def own(ref, level, reach):
        nx, ny = dims[level]
        return ref.at[pl.ds(reach, nx), pl.ds(reach, ny)]

    loads = [None] * LEVELS
    for level in reversed(range(LEVELS)):
        loads[level] = [
            fetch(shifts[level], H[level]),
            fetch(guesses[level], own(U[level], level, REACH)),
            fetch(sources[level], own(S[level], level, REACH - 1)),
        ]
    block_loads = [None] * (LEVELS - 1)
    for level in reversed(range(LEVELS - 1)):
        block_loads[level] = fetch(blocks[level], B[level])

    for level in reversed(range(LEVELS)):
        nx, ny = dims[level]
        for copy in loads[level]:
            copy.wait()
        for i in range(nx):
            for j in range(ny):
                D[level][i + REACH - 1, j + REACH - 1] = 6.0 + H[level][i, pl.ds(j, 1)]

    pl.semaphore_wait(barrier, len(company))

    counter = Counter()
    pending = []

    def exchange(ref, level, reach, box=False):
        copies = []
        for ox, oy, source, target, size in plan(*dims[level], reach, box):
            index = counter.take()
            copy = pltpu.make_async_remote_copy(
                src_ref=ref.at[pl.ds(source[0] + reach, size[0]), pl.ds(source[1] + reach, size[1])],
                dst_ref=ref.at[pl.ds(target[0] + reach, size[0]), pl.ds(target[1] + reach, size[1])],
                send_sem=send_sem.at[index],
                recv_sem=recv_sem.at[index],
                device_id=at(ox, oy),
                device_id_type=pl.DeviceIdType.MESH,
            )
            copy.start()
            copies.append(copy)
        pending.extend(copies)
        return copies

    first, steps = coefficients()

    def rows(count, body):
        if count <= 5:
            for i in range(count):
                body(i)
        else:
            lax.fori_loop(0, count, lambda i, c: (body(i), c)[1], 0)

    def operate(ref, diagonal, i, count):
        wide = ref[i + 1]
        middle = wide[1 : count + 1]
        beside = wide[0:count] + wide[2 : count + 2]
        beside = beside + (ref[i, pl.ds(1, count)] + ref[i + 2, pl.ds(1, count)])
        beside = beside + (pltpu.roll(middle, 1, 2) + pltpu.roll(middle, middle.shape[2] - 1, 2))
        return diagonal * middle - beside

    def smooth(level):
        nx, ny = dims[level]
        u, s, d, r, p0, p1, o = (x[level] for x in (U, S, D, R, P0, P1, O))

        def start(i):
            residual = s[i] - operate(u, d[i], i, ny + 4)
            r[i] = residual
            p0[i] = residual * first

        rows(nx + 4, start)
        ahead, along = steps[0]

        def second(i):
            residual = r[i + 1, pl.ds(1, ny + 2)] - operate(p0, d[i + 1, pl.ds(1, ny + 2)], i, ny + 2)
            r[i + 1, pl.ds(1, ny + 2)] = residual
            p1[i] = ahead * p0[i + 1, pl.ds(1, ny + 2)] + along * residual

        rows(nx + 2, second)
        again, around = steps[1]

        def third(i):
            residual = r[i + 2, pl.ds(2, ny)] - operate(p1, d[i + 2, pl.ds(2, ny)], i, ny)
            direction = p1[i + 1, pl.ds(1, ny)]
            last = again * direction + around * residual
            result = u[i + 3, pl.ds(3, ny)] + p0[i + 2, pl.ds(2, ny)] + direction + last
            o[i] = result
            if level:
                C[level - 1][i + 1, pl.ds(1, ny)] = result.astype(jnp.bfloat16)

        rows(nx, third)
        return fetch(o, outs[level])

    def prolong(level):
        nx, ny = dims[level]
        cx, cy = dims[level + 1]
        full = (cx * peers[0], cy * peers[1])
        lift_x = full[0] + 1 - gz * cx
        lift_y = full[1] + 1 - gy * cy

        def pick(i, j, k):
            link = links[level][i, j, k]
            row = modulo(quotient(link, full[1]) + lift_x, full[0])
            col = modulo(modulo(link, full[1]) + lift_y, full[1])
            return C[level][jnp.minimum(row, cx + 1), jnp.minimum(col, cy + 1)]

        def body(i):
            for j in range(ny):
                picked = jnp.concatenate([pick(i, j, 0), pick(i, j, 1)], axis=1)
                block = jnp.concatenate([B[level][i, j, 0], B[level][i, j, 1]], axis=1)
                sums = lax.dot_general(
                    picked, block, (((1,), (1,)), ((), ())), preferred_element_type=jnp.float32
                )
                U[level][i + REACH, j + REACH] = U[level][i + REACH, j + REACH] + sums

        rows(nx, body)

    ready = exchange(U[3], 3, REACH)
    sides = [None] * LEVELS
    for level in reversed(range(1, LEVELS)):
        sides[level] = exchange(S[level], level, REACH - 1) + exchange(D[level], level, REACH - 1)
    stores = []
    for level in reversed(range(LEVELS)):
        if level < LEVELS - 1:
            block_loads[level].wait()
            prolong(level)
            ready = exchange(U[level], level, REACH)
        for copy in ready + sides[level]:
            copy.wait_recv()
        if level == 2:
            sides[0] = exchange(S[0], 0, REACH - 1) + exchange(D[0], 0, REACH - 1)
        stores.append(smooth(level))
        if level:
            for copy in exchange(C[level - 1], level, 1, True):
                copy.wait_recv()
    for copy in pending:
        copy.wait_send()
    for copy in stores:
        copy.wait()


def shards(peers, *args):
    dims = [x.shape[:2] for x in args[:4]]
    line = args[0].shape[2:]
    width = line[1:]

    def level_scratch(extra, shape):
        return [pltpu.VMEM((nx + extra, ny + extra) + shape, jnp.float32) for nx, ny in dims]

    scratch = (
        level_scratch(2 * REACH, line)
        + level_scratch(2 * REACH - 2, line)
        + level_scratch(2 * REACH - 2, (1,) + width)
        + level_scratch(2 * REACH - 2, line)
        + level_scratch(2 * REACH - 2, line)
        + level_scratch(2 * REACH - 4, line)
        + level_scratch(0, line)
        + [pltpu.VMEM(x.shape, x.dtype) for x in args[12:15]]
        + [pltpu.VMEM((nx + 2, ny + 2) + line, jnp.bfloat16) for nx, ny in dims[1:]]
        + level_scratch(0, width)
    )
    messages = message_count(dims)
    scratch += [
        pltpu.SemaphoreType.DMA((24,)),
        pltpu.SemaphoreType.DMA((messages,)),
        pltpu.SemaphoreType.DMA((messages,)),
    ]
    anywhere = pl.BlockSpec(memory_space=pl.ANY)
    outs = pl.pallas_call(
        partial(kernel, dims, peers),
        out_shape=[jax.ShapeDtypeStruct(x.shape, x.dtype) for x in args[:4]],
        in_specs=[anywhere] * 15 + [pl.BlockSpec(memory_space=pltpu.SMEM)] * 3,
        out_specs=[anywhere] * 4,
        scratch_shapes=scratch,
        compiler_params=pltpu.CompilerParams(
            collective_id=0, has_side_effects=True, vmem_limit_bytes=67043328
        ),
    )(*args)
    return tuple(outs)


def solution(mesh):
    peers = (mesh.shape["gz"], mesh.shape["gy"])
    grid = P("gz", "gy")
    return jax.shard_map(
        partial(shards, peers),
        mesh=mesh,
        in_specs=(grid,) * 18,
        out_specs=(grid,) * 4,
        check_vma=False,
    )
```

profile of v0, /device:TPU:0, one launch (start us, length us, event | category | flops | bytes accessed | tf_op | source)
XLA Modules:
  0.0 82.1 jit_solution(6544067177829204933)
XLA Ops:
  0.6 1.4 %copy.23.refs_16_ = s32[4,4,2]{2,1,0:T(4,128)} copy(s32[4,4,2]{1,2,0:T(2,128)} %param.34) | data formatting | bytes 256 | tf_op args[16]
  2.0 1.4 %copy.22.refs_15_ = s32[8,8,2]{2,1,0:T(8,128)} copy(s32[8,8,2]{1,2,0:T(2,128)} %param.33) | data formatting | bytes 1024 | tf_op args[15]
  3.4 72.6 %shard_map.201 = (f32[8,8,16,128]{3,2,1,0:T(8,128)}, f32[4,4,16,128]{3,2,1,0:T(8,128)}, f32[2,2,16,128]{3,2,1,0:T(8,128)}, f32[1,1,16,128]{3,2,1,0:T(8,128)}) custom-call(f32[8,8,16,128]{3,2,1,0:T(8,128)} %refs_0_.1, f32[4,4,16,128]{3,2,1,0:T(8,128)} %refs_1_.1, f32[2,2,16,128]{3,2,1,0:T(8,128)} %refs_2_.1, f32[1,1,16,128]{3,2,1,0:T(8,128)} %refs_3_.1, ...), custom_call_target="tpu_custom_call" | custom-call | tf_op jit(solution)/shard_map/pallas_call | solution.py:289
  76.0 1.9 %copy.28 = f32[8,8,16,128]{3,2,1,0:T(8,128)} copy(f32[8,8,16,128]{3,2,1,0:T(8,128)} %get-tuple-element.8) | data formatting | bytes 1048576
  77.9 1.6 %copy.29 = f32[4,4,16,128]{3,2,1,0:T(8,128)} copy(f32[4,4,16,128]{3,2,1,0:T(8,128)} %get-tuple-element.9) | data formatting | bytes 262144
  79.5 1.4 %copy.30 = f32[2,2,16,128]{3,2,1,0:T(8,128)} copy(f32[2,2,16,128]{3,2,1,0:T(8,128)} %get-tuple-element.10) | data formatting | bytes 65536
  80.8 1.3 %copy.31 = f32[1,1,16,128]{3,2,1,0:T(8,128)} copy(f32[1,1,16,128]{3,2,1,0:T(8,128)} %get-tuple-element.11) | data formatting | bytes 16384
where the time goes:
time: 82.6 us; the launch traced here: 82.1 us
  Pallas kernels  72.6 us (88%)
  local copies, waits for them, and re-layouts  8.91 us (11%)
    pallas_call x1, Pallas kernels, shards(): pl.pallas_call(partial(kernel, dims, peers), out_shape=[jax.ShapeDtypeStr...  72.6 us
    unnamed x6, local copies, waits for them, and re-layouts  8.91 us

commit v1 on v0

v1 whole, which is shorter than its diff:
```python
from functools import partial

import jax
import jax.numpy as jnp
from jax import lax
from jax.experimental import pallas as pl
from jax.experimental.pallas import tpu as pltpu
from jax.sharding import PartitionSpec as P

LEVELS = 4
REACH = 3
LAST = LEVELS - 1

upper_edge = 14.0
lower_edge = upper_edge / 8.0


def coefficients():
    centre = (upper_edge + lower_edge) / 2.0
    half_width = (upper_edge - lower_edge) / 2.0
    ratio = centre / half_width
    factor = 1.0 / ratio
    steps = []
    for _ in range(2):
        following = 1.0 / (2.0 * ratio - factor)
        steps.append((following * factor, 2.0 * following / half_width))
        factor = following
    (a1, b1), (a2, b2) = steps
    first = 1.0 / centre
    return {
        "own1": first * (a1 + b1 * centre),
        "side1": first * b1,
        "start2": first * (1.0 - a1 * b2 / b1),
        "own2": 1.0 + a2 + b2 / b1,
        "side2": b2,
    }


def beyond(index, length):
    return max(-index, index - length + 1, 0)


def plan(nx, ny, reach, box=False):
    def width(row):
        return reach if box else reach - beyond(row, nx)

    out = []
    far_x, far_y = -(-reach // nx), -(-reach // ny)
    for ox in range(-far_x, far_x + 1):
        for oy in range(-far_y, far_y + 1):
            if ox == 0 and oy == 0:
                continue
            runs = []
            for row in range(max(-ox * nx, -reach), min((1 - ox) * nx, nx + reach)):
                low = max(-oy * ny, -width(row))
                high = min((1 - oy) * ny, ny + width(row))
                if low >= high:
                    continue
                if runs and runs[-1][2:] == (low, high) and runs[-1][1] == row:
                    runs[-1] = (runs[-1][0], row + 1, low, high)
                else:
                    runs.append((row, row + 1, low, high))
            for top, end, low, high in runs:
                out.append(
                    (ox, oy, (top + ox * nx, low + oy * ny), (top, low), (end - top, high - low))
                )
    out.sort(key=lambda m: (-abs(m[0]), -abs(m[1]), m))
    return out


class Gather:
    def __init__(self, block, peers):
        self.block, self.peers = block, peers
        self.size = (block[0] * peers[0], block[1] * peers[1])
        self.u = self.around(3)
        self.s = self.around(2)
        self.slot = {cell: k for k, cell in enumerate(self.u)}

    def at(self, x, y):
        return x % self.size[0], y % self.size[1]

    def around(self, reach):
        nx, ny = self.block
        cells = []
        for x in range(-reach - 1, nx + reach + 1):
            for y in range(-reach - 1, ny + reach + 1):
                far = max(beyond(x, nx) - 1, 0) + max(beyond(y, ny) - 1, 0)
                if far <= reach and self.at(x, y) not in cells:
                    cells.append(self.at(x, y))
        return cells

    def messages(self):
        nx, ny = self.block

        def span(offset, count):
            return min(offset, count - offset)

        out = []
        for cell in self.u:
            ox, oy = cell[0] // nx, cell[1] // ny
            if ox or oy:
                own = self.slot[(cell[0] % nx, cell[1] % ny)]
                far = span(ox, self.peers[0]) + span(oy, self.peers[1])
                out.append((-far, -ox, -oy, own, self.slot[cell], cell in self.s))
        out.sort()
        return [m[1:] for m in out]


def modulo(value, size):
    if size & (size - 1) == 0:
        return jnp.bitwise_and(value, size - 1)
    return lax.rem(value, size)


def quotient(value, size):
    if size & (size - 1) == 0:
        return jnp.right_shift(value, size.bit_length() - 1)
    return lax.div(value, size)


class Counter:
    def __init__(self):
        self.used = 0

    def take(self):
        self.used += 1
        return self.used - 1


def message_count(dims, peers):
    total = 4 + sum(1 + 2 * m[-1] for m in Gather(dims[LAST], peers).messages())
    for level, (nx, ny) in enumerate(dims[:LAST]):
        total += len(plan(nx, ny, REACH)) + 2 * len(plan(nx, ny, REACH - 1))
        if level:
            total += len(plan(nx, ny, 1, True))
    return total


def partners(dims, peers):
    found = set()
    for nx, ny in dims[:LAST]:
        for m in plan(nx, ny, REACH) + plan(nx, ny, 1, True):
            found.add((m[0] % peers[0], m[1] % peers[1]))
            found.add((-m[0] % peers[0], -m[1] % peers[1]))
    for m in Gather(dims[LAST], peers).messages():
        found.add((m[0] % peers[0], m[1] % peers[1]))
        found.add((-m[0] % peers[0], -m[1] % peers[1]))
    return sorted(found)


def turned(shape):
    return shape[1] > shape[2]


def beside(centre, above, below):
    middle = centre[1:-1]
    line = middle.shape[-1]
    total = (centre[:-2] + centre[2:]) + (above + below)
    return total + (pltpu.roll(middle, 1, 3) + pltpu.roll(middle, line - 1, 3))


def smoothing(nx, ny, u, s, w0, w1, w2, q, p, finish):
    k = coefficients()

    def start(row):
        w = 2 - beyond(row, nx)
        count = ny + 2 * w
        near = beside(
            u[row + 3, pl.ds(2 - w, count + 2)],
            u[row + 2, pl.ds(3 - w, count)],
            u[row + 4, pl.ds(3 - w, count)],
        )
        own = u[row + 3, pl.ds(3 - w, count)]
        weight = w0[row + 2, pl.ds(2 - w, count)][:, None]
        q[row + 2, pl.ds(2 - w, count)] = (s[row + 2, pl.ds(2 - w, count)] - weight * own) + near

    def second(row):
        w = 1 - beyond(row, nx)
        count = ny + 2 * w
        near = beside(
            q[row + 2, pl.ds(1 - w, count + 2)],
            q[row + 1, pl.ds(2 - w, count)],
            q[row + 3, pl.ds(2 - w, count)],
        )
        own = q[row + 2, pl.ds(2 - w, count)]
        weight = w1[row + 1, pl.ds(1 - w, count)][:, None]
        p[row + 1, pl.ds(1 - w, count)] = weight * own + k["side1"] * near

    def third(row):
        near = beside(
            p[row + 1, pl.ds(0, ny + 2)], p[row, pl.ds(1, ny)], p[row + 2, pl.ds(1, ny)]
        )
        own = p[row + 1, pl.ds(1, ny)]
        begin = u[row + 3, pl.ds(3, ny)] + k["start2"] * q[row + 2, pl.ds(2, ny)]
        finish(row, (begin + w2[row][:, None] * own) + k["side2"] * near)

    for row in range(-2, nx + 6):
        if row < nx + 2:
            start(row)
        if -1 <= row - 2 < nx + 1:
            second(row - 2)
        if 0 <= row - 4 < nx:
            third(row - 4)


def upward(dims, peers, *refs):
    refs = list(refs)

    def take(count):
        got = refs[:count]
        del refs[:count]
        return got

    sources, guesses, shifts = take(4), take(4), take(4)
    blocks, link_inputs = take(3), take(3)
    start_out, source_out, w0_out, w1_out, w2_out = take(5)
    outs = [None] + take(3)
    U, S = [start_out] + take(2), [source_out] + take(2)
    D, H = take(3), take(4)
    W0, W1, W2 = [w0_out] + take(2), [w1_out] + take(2), [w2_out] + take(2)
    Q, PD = [None] + take(2), [None] + take(2)
    V, T, W = take(3)
    B, BT, C = take(3), take(3), take(3)
    K, DK, QK, PK = take(4)
    links = take(3)
    local_sem, send_sem, recv_sem = take(3)
    gz, gy = lax.axis_index("gz"), lax.axis_index("gy")
    k = coefficients()

    def at(ox, oy):
        return (lax.rem(gz + (ox % peers[0]), peers[0]), lax.rem(gy + (oy % peers[1]), peers[1]))

    barrier = pltpu.get_barrier_semaphore()
    company = partners(dims, peers)
    for ox, oy in company:
        pl.semaphore_signal(barrier, inc=1, device_id=at(ox, oy), device_id_type=pl.DeviceIdType.MESH)

    local = Counter()

    def fetch(source, target):
        copy = pltpu.make_async_copy(source, target, local_sem.at[local.take()])
        copy.start()
        return copy

    gather = Gather(dims[LAST], peers)
    last_x, last_y = dims[LAST]
    own_cells = [(x, y) for x in range(last_x) for y in range(last_y)]
    loads = [None] * LEVELS
    loads[LAST] = [fetch(shifts[LAST], H[LAST])]
    for x, y in own_cells:
        slot = gather.slot[(x, y)]
        loads[LAST].append(fetch(guesses[LAST].at[x, y], K.at[slot, 0]))
        loads[LAST].append(fetch(sources[LAST].at[x, y], K.at[slot, 1]))

    def own(ref, level, reach):
        nx, ny = dims[level]
        return ref.at[pl.ds(reach, nx), pl.ds(reach, ny)]

    for level in reversed(range(LAST)):
        loads[level] = [
            fetch(shifts[level], H[level]),
            fetch(sources[level], own(S[level], level, REACH - 1)),
            fetch(guesses[level], own(U[level], level, REACH)),
        ]
    for level in reversed(range(LAST)):
        loads[level].append(fetch(link_inputs[level], links[level]))
    block_loads = [None] * LAST
    for level in reversed(range(LAST)):
        block_loads[level] = fetch(blocks[level], B[level])

    for copy in loads[LAST]:
        copy.wait()
    for x, y in own_cells:
        DK[gather.slot[(x, y)]] = 6.0 + H[LAST][x, pl.ds(y, 1)]

    pl.semaphore_wait(barrier, len(company))

    counter = Counter()
    pending = []

    def send(source, target, device, later=True):
        index = counter.take()
        copy = pltpu.make_async_remote_copy(
            src_ref=source,
            dst_ref=target,
            send_sem=send_sem.at[index],
            recv_sem=recv_sem.at[index],
            device_id=device,
            device_id_type=pl.DeviceIdType.MESH,
        )
        copy.start()
        if later:
            pending.append(copy)
        return copy

    def rectangle(ref, corner, size, pad):
        return ref.at[pl.ds(corner[0] + pad, size[0]), pl.ds(corner[1] + pad, size[1])]

    def exchange(ref, pad, messages):
        return [
            send(rectangle(ref, source, size, pad), rectangle(ref, target, size, pad), at(ox, oy))
            for ox, oy, source, target, size in messages
        ]

    last = []
    for ox, oy, source, target, whole in gather.messages():
        if whole:
            last.append(send(K.at[source], K.at[target], at(ox, oy)))
            last.append(send(DK.at[source], DK.at[target], at(ox, oy)))
        else:
            last.append(send(K.at[source, 0], K.at[target, 0], at(ox, oy)))

    def diagonals(level):
        nx, ny = dims[level]
        for copy in loads[level]:
            copy.wait()
        for i in range(nx):
            for j in range(ny):
                D[level][i + 2, j + 2] = 6.0 + H[level][i, pl.ds(j, 1)]

    def sides(level, narrow=None):
        messages = plan(*dims[level], REACH - 1)
        copies = []
        for m in messages:
            ref = S[level] if narrow is None or m[0] == 0 else narrow
            copies += exchange(ref, 2, [m])
        return copies + exchange(D[level], 2, messages)

    def weigh(level):
        nx, ny = dims[level]
        for row in range(-2, nx + 2):
            w = 2 - beyond(row, nx)
            for col in range(-w, ny + w):
                d = jnp.broadcast_to(D[level][row + 2, col + 2], W0[level].shape[2:])
                W0[level][row + 2, col + 2] = d
                far = beyond(row, nx) + beyond(col, ny)
                if far <= 1:
                    W1[level][row + 1, col + 1] = k["own1"] - k["side1"] * d
                if far == 0:
                    W2[level][row, col] = k["own2"] - k["side2"] * d

    def turn(level):
        nx, ny = dims[level]
        block_loads[level].wait()
        line = B[level].shape[-1]

        def body(cell, carry):
            i, j = cell // ny, cell % ny
            for side in range(2):
                BT[level][i, j, pl.ds(side * line, line)] = B[level][i, j, side].T
            return carry

        lax.fori_loop(0, nx * ny, body, 0)

    def smooth(level):
        nx, ny = dims[level]

        def finish(row, result):
            outs[level][row] = result
            lines = result.reshape(result.shape[:1] + C[level - 1].shape[2:])
            C[level - 1][row + 1, pl.ds(1, ny)] = lines.astype(jnp.bfloat16)

        smoothing(
            nx, ny, U[level], S[level], W0[level], W1[level], W2[level], Q[level], PD[level], finish
        )

    def smooth_last():
        def near(ref, x, y):
            def cell(a, b):
                return ref[gather.slot[gather.at(a, b)]]

            middle = cell(x, y)
            total = (cell(x, y - 1) + cell(x, y + 1)) + (cell(x - 1, y) + cell(x + 1, y))
            line = middle.shape[-1]
            return middle, total + (pltpu.roll(middle, 1, 2) + pltpu.roll(middle, line - 1, 2))

        for x, y in gather.around(2):
            slot = gather.slot[(x, y)]
            middle, total = near(K.at[:, 0], x, y)
            QK[slot] = (K[slot, 1] - DK[slot] * middle) + total
        for x, y in gather.around(1):
            slot = gather.slot[(x, y)]
            middle, total = near(QK, x, y)
            PK[slot] = (k["own1"] - k["side1"] * DK[slot]) * middle + k["side1"] * total
        for x in range(-1, last_x + 1):
            for y in range(-1, last_y + 1):
                slot = gather.slot[gather.at(x, y)]
                middle, total = near(PK, x, y)
                begin = K[slot, 0] + k["start2"] * QK[slot]
                result = begin + (k["own2"] - k["side2"] * DK[slot]) * middle + k["side2"] * total
                if (x, y) in own_cells:
                    outs[LAST][x, y] = result
                C[LAST - 1][x + 1, y + 1] = result.reshape(C[LAST - 1].shape[2:]).astype(jnp.bfloat16)

    def prolong(level, rows):
        nx, ny = dims[level]
        cx, cy = dims[level + 1]
        full = (cx * peers[0], cy * peers[1])
        lift_x = full[0] + 1 - gz * cx
        lift_y = full[1] + 1 - gy * cy

        def pick(i, j, side):
            if turned((nx, ny, 2)):
                link = links[level][i, side, j]
            else:
                link = links[level][i, j, side]
            row = modulo(quotient(link, full[1]) + lift_x, full[0])
            col = modulo(modulo(link, full[1]) + lift_y, full[1])
            return C[level][jnp.minimum(row, cx + 1), jnp.minimum(col, cy + 1)]

        for i in rows:
            for j in range(ny):
                picked = jnp.concatenate([pick(i, j, 0), pick(i, j, 1)], axis=1)
                sums = lax.dot_general(
                    picked, BT[level][i, j], (((1,), (0,)), ((), ())), preferred_element_type=jnp.float32
                )
                u = U[level][i + REACH, j + REACH]
                u = u + sums.reshape(u.shape)
                U[level][i + REACH, j + REACH] = u
                if level == 0:
                    V[i + REACH, j + REACH] = u.reshape(sums.shape).astype(jnp.bfloat16)
                    if i == 0:
                        W[0, j] = sums.astype(jnp.bfloat16)
                    if i == nx - 1:
                        W[1, j] = sums.astype(jnp.bfloat16)

    def widen(source, target, pad, corner, size):
        for row in range(corner[0] + pad, corner[0] + pad + size[0]):
            cells = pl.ds(corner[1] + pad, size[1])
            value = source[row, cells].astype(jnp.float32)
            target[row, cells] = value.reshape(value.shape[:1] + target.shape[2:])

    diagonals(2)
    side2 = sides(2)
    diagonals(1)
    diagonals(0)
    nx, ny = dims[0]
    for i in range(nx):
        value = S[0][i + 2, pl.ds(2, ny)]
        T[i + 2, pl.ds(2, ny)] = value.reshape(value.shape[:1] + T.shape[2:]).astype(jnp.bfloat16)
    for level in reversed(range(LAST)):
        turn(level)

    def wait(copies):
        for copy in copies:
            copy.wait_recv()

    wait(last)
    smooth_last()
    prolong(2, range(dims[2][0]))
    begin2 = exchange(U[2], REACH, plan(*dims[2], REACH))
    side1 = sides(1)
    wait(side2)
    weigh(2)
    wait(begin2)
    smooth(2)
    coarse1 = exchange(C[1], 1, plan(*dims[2], 1, True))
    side0 = sides(0, T)
    wait(side1)
    weigh(1)
    wait(coarse1)
    prolong(1, range(dims[1][0]))
    begin1 = exchange(U[1], REACH, plan(*dims[1], REACH))
    messages = plan(*dims[0], REACH - 1)
    wait(side0)
    for m in messages:
        if m[0]:
            widen(T, S[0], 2, m[3], m[4])
    weigh(0)
    wait(begin1)
    smooth(1)
    coarse0 = exchange(C[0], 1, plan(*dims[1], 1, True))
    edges = ((1, nx - 1, -1, 1, 2), (-1, 0, nx, 0, 3))
    early = []
    for ox, row, place, _, _ in edges:
        cells = pl.ds(REACH, ny)
        source = U[0].at[row + REACH, cells]
        early.append(send(source, U[0].at[place + REACH, cells], at(ox, 0), False))
    wait(coarse0)
    for copy in early:
        copy.wait_send()

    messages = []
    for ox, oy, source, target, size in plan(*dims[0], REACH):
        if ox and not oy:
            shift = 1 if ox < 0 else 0
            source, target = (source[0] + shift, source[1]), (target[0] + shift, target[1])
            size = (size[0] - 1, size[1])
        messages.append((ox, oy, source, target, size))
    begin0 = []
    slim = []
    done = set()
    for rows in (range(min(REACH, nx)), range(max(nx - REACH, 0), nx), range(nx)):
        fresh = [i for i in rows if i not in done]
        done.update(fresh)
        prolong(0, fresh)
        for ox, row, place, slot, landing in edges:
            if row in fresh:
                slim.append((place, landing, send(W.at[slot], W.at[landing], at(ox, 0))))
        ready = [m for m in messages if all(m[2][0] + i in done for i in range(m[4][0]))]
        messages = [m for m in messages if m not in ready]
        for m in ready:
            begin0.append((m, exchange(V if m[0] else U[0], REACH, [m])[0]))
    wait(early)
    for place, landing, copy in slim:
        copy.wait_recv()
        value = W[landing].astype(jnp.float32)
        guess = U[0][place + REACH, pl.ds(REACH, ny)]
        U[0][place + REACH, pl.ds(REACH, ny)] = guess + value.reshape(guess.shape)
    for m, copy in begin0:
        copy.wait_recv()
        if m[0]:
            widen(V, U[0], REACH, m[3], m[4])
    for copy in pending:
        copy.wait_send()


def finishing(nx, ny, *refs):
    u, s, w0, w1, w2 = refs[:5]
    values, outs = refs[5:8], refs[8:12]
    q, p, o, sem = refs[12:]
    copies = []

    def store(source, target):
        copy = pltpu.make_async_copy(source, target, sem.at[len(copies)])
        copy.start()
        copies.append(copy)

    for value, out in zip(values, outs[1:]):
        store(value, out)

    def finish(row, result):
        o[row] = result
        store(o.at[row], outs[0].at[row])

    smoothing(nx, ny, u, s, w0, w1, w2, q, p, finish)
    for copy in copies:
        copy.wait()


def shards(peers, *args):
    dims = [x.shape[:2] for x in args[:4]]
    sides, width = args[0].shape[2:]
    tile = (8, width)
    line = (sides // 8,) + tile
    packed = (sides, width)
    args = [x.reshape(x.shape[:2] + line) for x in args[:8]] + list(args[8:])
    for n in range(15, 18):
        if turned(args[n].shape):
            args[n] = jnp.swapaxes(args[n], 1, 2)

    args = [pltpu.with_memory_space_constraint(x, pltpu.HBM) for x in args]

    def grown(level, extra, shape, dtype=jnp.float32):
        nx, ny = dims[level]
        return (nx + extra, ny + extra) + shape, dtype

    middle = (1, 2)
    results = [
        grown(0, 2 * REACH, line),
        grown(0, 4, line),
        grown(0, 4, tile),
        grown(0, 2, tile),
        grown(0, 0, tile),
    ] + [grown(level, 0, line) for level in (1, 2, 3)]
    slots = len(Gather(dims[LAST], peers).u)
    scratch = (
        [grown(n, 2 * REACH, line) for n in middle]
        + [grown(n, 4, line) for n in middle]
        + [grown(n, 4, (1, width)) for n in range(LAST)]
        + [grown(n, 0, (width,)) for n in range(LEVELS)]
        + [grown(n, 4, tile) for n in middle]
        + [grown(n, 2, tile) for n in middle]
        + [grown(n, 0, tile) for n in middle]
        + [grown(n, 4, line) for n in middle]
        + [grown(n, 2, line) for n in middle]
        + [grown(0, 2 * REACH, packed, jnp.bfloat16), grown(0, 4, packed, jnp.bfloat16)]
        + [((4, dims[0][1]) + packed, jnp.bfloat16)]
        + [(x.shape, x.dtype) for x in args[12:15]]
        + [(x.shape[:2] + (2 * width, width), x.dtype) for x in args[12:15]]
        + [grown(n, 2, packed, jnp.bfloat16) for n in range(1, LEVELS)]
        + [
            ((slots, 2) + line, jnp.float32),
            ((slots, 1, width), jnp.float32),
            ((slots,) + line, jnp.float32),
            ((slots,) + line, jnp.float32),
        ]
    )
    messages = message_count(dims, peers)
    anywhere = pl.BlockSpec(memory_space=pl.ANY)
    inside = pl.BlockSpec(memory_space=pltpu.VMEM)
    held = pl.pallas_call(
        partial(upward, dims, peers),
        out_shape=[pltpu.VMEM(*r) for r in results],
        in_specs=[anywhere] * 18,
        out_specs=[inside] * len(results),
        scratch_shapes=[pltpu.VMEM(*x) for x in scratch]
        + [pltpu.SMEM(x.shape, x.dtype) for x in args[15:]]
        + [
            pltpu.SemaphoreType.DMA((32,)),
            pltpu.SemaphoreType.DMA((messages,)),
            pltpu.SemaphoreType.DMA((messages,)),
        ],
        compiler_params=pltpu.CompilerParams(
            collective_id=0, has_side_effects=True, vmem_limit_bytes=40 * 2**20
        ),
    )(*args)
    nx, ny = dims[0]
    outs = pl.pallas_call(
        partial(finishing, nx, ny),
        out_shape=[jax.ShapeDtypeStruct(d + line, jnp.float32) for d in dims],
        in_specs=[inside] * len(results),
        out_specs=[anywhere] * LEVELS,
        scratch_shapes=[
            pltpu.VMEM(*grown(0, 4, line)),
            pltpu.VMEM(*grown(0, 2, line)),
            pltpu.VMEM(*grown(0, 0, line)),
            pltpu.SemaphoreType.DMA((nx + LEVELS,)),
        ],
        compiler_params=pltpu.CompilerParams(vmem_limit_bytes=16 * 2**20),
    )(*held)
    return tuple(x.reshape(x.shape[:2] + packed) for x in outs)


def solution(mesh):
    peers = (mesh.shape["gz"], mesh.shape["gy"])
    grid = P("gz", "gy")
    return jax.shard_map(
        partial(shards, peers),
        mesh=mesh,
        in_specs=(grid,) * 18,
        out_specs=(grid,) * 4,
        check_vma=False,
    )
```

time: 82.6 us -> 57.7 us (0.70)
  Pallas kernels: 72.6 us -> 56.9 us
  local copies, waits for them, and re-layouts: 8.91 us -> 0 us
    pallas_call x1 -> x2, Pallas kernels: 72.6 us -> 56.9 us  [the longest x1 54.6 us: shards(): pl.pallas_call(partial(upward, dims, peers), out_shape=[pltpu.VMEM(*r) fo...]
    unnamed x6 -> x0, local copies, waits for them, and re-layouts: 8.91 us -> none
where the time goes in v1:
time: 57.7 us; the launch traced here: 57.5 us
  Pallas kernels  56.9 us (99%)
  between operations  0.65 us (1%)
    pallas_call x1, Pallas kernels, shards(): pl.pallas_call(partial(upward, dims, peers), out_shape=[pltpu.VMEM(*r) fo...  54.6 us
    pallas_call x1, Pallas kernels, shards(): pl.pallas_call(partial(finishing, nx, ny), out_shape=[jax.ShapeDtypeStruc...  2.24 us

profile of v1, /device:TPU:0, one launch (start us, length us, event | category | flops | bytes accessed | tf_op | source)
XLA Modules:
  0.0 57.5 jit_solution(11672967583027787829)
XLA Ops:
  0.6 54.6 %shard_map.201 = (f32[14,14,2,8,128]{4,3,2,1,0:T(8,128)S(1)}, f32[12,12,2,8,128]{4,3,2,1,0:T(8,128)S(1)}, f32[12,12,8,128]{3,2,1,0:T(8,128)S(1)}, f32[10,10,8,12...) custom-call(f32[8,8,2,8,128]{4,3,2,1,0:T(8,128)} %bitcast.14, ...), custom_call_target="tpu_custom_call" | custom-call | tf_op jit(solution)/shard_map/pallas_call | solution.py:592
  55.3 2.2 %shard_map.202 = (f32[8,8,2,8,128]{4,3,2,1,0:T(8,128)}, f32[4,4,2,8,128]{4,3,2,1,0:T(8,128)}, f32[2,2,2,8,128]{4,3,2,1,0:T(8,128)}, f32[1,1,2,8,128]{4,3,2,1,0:T(8,128)}) custom-call(f32[14,14,2,8,128]{4,3,2,1,0:T(8,128)S(1)} %get-tuple-element.16.refs_0_, f32[12,12,2,8,128]{4,3,2,1,0:T(8,128)S(1)} %get-tuple-element.17.refs_1_, ...), custom_call_target="tpu_custom_call" | custom-call | tf_op jit(solution)/shard_map/pallas_call | solution.py:609

commit v2 on v1

--- a/solution.py
+++ b/solution.py
@@ -69,39 +69,28 @@
 
 
 class Gather:
-    def __init__(self, block, peers):
-        self.block, self.peers = block, peers
-        self.size = (block[0] * peers[0], block[1] * peers[1])
-        self.u = self.around(3)
-        self.s = self.around(2)
-        self.slot = {cell: k for k, cell in enumerate(self.u)}
-
-    def at(self, x, y):
-        return x % self.size[0], y % self.size[1]
+    def __init__(self, peers):
+        self.size = peers
+        rows = {x % peers[0]: abs(x) for x in (4, -4, 3, -3, 2, -2, 1, -1, 0)}
+        self.far = {x: min(x, peers[0] - x) for x in rows}
+        self.row = {x: k for k, x in enumerate(sorted(rows))}
 
     def around(self, reach):
-        nx, ny = self.block
         cells = []
-        for x in range(-reach - 1, nx + reach + 1):
-            for y in range(-reach - 1, ny + reach + 1):
-                far = max(beyond(x, nx) - 1, 0) + max(beyond(y, ny) - 1, 0)
-                if far <= reach and self.at(x, y) not in cells:
-                    cells.append(self.at(x, y))
+        for x in range(-reach - 1, reach + 2):
+            for y in range(-reach - 1, reach + 2):
+                far = max(abs(x) - 1, 0) + max(abs(y) - 1, 0)
+                cell = (x % self.size[0], y % self.size[1])
+                if far <= reach and cell not in cells:
+                    cells.append(cell)
         return cells
 
     def messages(self):
-        nx, ny = self.block
-
-        def span(offset, count):
-            return min(offset, count - offset)
-
         out = []
-        for cell in self.u:
-            ox, oy = cell[0] // nx, cell[1] // ny
-            if ox or oy:
-                own = self.slot[(cell[0] % nx, cell[1] % ny)]
-                far = span(ox, self.peers[0]) + span(oy, self.peers[1])
-                out.append((-far, -ox, -oy, own, self.slot[cell], cell in self.s))
+        for x in self.row:
+            for y in range(0, self.size[1], 2):
+                if x or y:
+                    out.append((-self.far[x] - min(y, self.size[1] - y), x, y, self.far[x] <= 3))
         out.sort()
         return [m[1:] for m in out]
 
@@ -127,12 +116,41 @@
         return self.used - 1
 
 
+def corners(nx, ny):
+    out = []
+    for ox in (1, -1):
+        for far in range(1, REACH):
+            target, source = (-far, nx - far) if ox > 0 else (nx - 1 + far, far - 1)
+            out.append((ox, target, source, REACH - far))
+    return out
+
+
+def straight(nx, ny):
+    near, rest = [], []
+    for ox, oy, source, target, size in plan(nx, ny, REACH):
+        if ox and oy:
+            continue
+        if not ox:
+            rest.append((ox, oy, source, target, size))
+            continue
+        for row in range(size[0]):
+            far = beyond(target[0] + row, nx)
+            group = near if far < REACH else rest
+            m = (ox, oy, (source[0] + row, source[1]), (target[0] + row, target[1]), (1, size[1]))
+            group.append(m)
+    near.sort(key=lambda m: beyond(m[3][0], nx))
+    rest.sort(key=lambda m: -abs(m[0]))
+    return near, rest
+
+
 def message_count(dims, peers):
-    total = 4 + sum(1 + 2 * m[-1] for m in Gather(dims[LAST], peers).messages())
+    total = 6 + 2 * sum(1 + m[-1] for m in Gather(peers).messages())
     for level, (nx, ny) in enumerate(dims[:LAST]):
         total += len(plan(nx, ny, REACH)) + 2 * len(plan(nx, ny, REACH - 1))
         if level:
-            total += len(plan(nx, ny, 1, True))
+            total += len(plan(nx, ny, 1, True)) + 4 * REACH
+        else:
+            total += 6 * REACH
     return total
 
 
@@ -142,9 +160,9 @@
         for m in plan(nx, ny, REACH) + plan(nx, ny, 1, True):
             found.add((m[0] % peers[0], m[1] % peers[1]))
             found.add((-m[0] % peers[0], -m[1] % peers[1]))
-    for m in Gather(dims[LAST], peers).messages():
-        found.add((m[0] % peers[0], m[1] % peers[1]))
-        found.add((-m[0] % peers[0], -m[1] % peers[1]))
+    for x, y, _ in Gather(peers).messages():
+        found.add((x, y))
+        found.add((-x % peers[0], -y % peers[1]))
     return sorted(found)
 
 
@@ -159,8 +177,11 @@
     return total + (pltpu.roll(middle, 1, 3) + pltpu.roll(middle, line - 1, 3))
 
 
-def smoothing(nx, ny, u, s, w0, w1, w2, q, p, finish):
+def smoothing(nx, ny, u, s, w0, w1, w2, q, p, finish, middle=None):
     k = coefficients()
+
+    def wanted(row, margin):
+        return middle is None or (margin <= row < nx - margin) == middle
 
     def start(row):
         w = 2 - beyond(row, nx)
@@ -172,34 +193,36 @@
         )
         own = u[row + 3, pl.ds(3 - w, count)]
         weight = w0[row + 2, pl.ds(2 - w, count)][:, None]
-        q[row + 2, pl.ds(2 - w, count)] = (s[row + 2, pl.ds(2 - w, count)] - weight * own) + near
+        q(row)[row + 2, pl.ds(2 - w, count)] = (s[row + 2, pl.ds(2 - w, count)] - weight * own) + near
 
     def second(row):
         w = 1 - beyond(row, nx)
         count = ny + 2 * w
         near = beside(
-            q[row + 2, pl.ds(1 - w, count + 2)],
-            q[row + 1, pl.ds(2 - w, count)],
-            q[row + 3, pl.ds(2 - w, count)],
+            q(row)[row + 2, pl.ds(1 - w, count + 2)],
+            q(row - 1)[row + 1, pl.ds(2 - w, count)],
+            q(row + 1)[row + 3, pl.ds(2 - w, count)],
         )
-        own = q[row + 2, pl.ds(2 - w, count)]
+        own = q(row)[row + 2, pl.ds(2 - w, count)]
         weight = w1[row + 1, pl.ds(1 - w, count)][:, None]
-        p[row + 1, pl.ds(1 - w, count)] = weight * own + k["side1"] * near
+        p(row)[row + 1, pl.ds(1 - w, count)] = weight * own + k["side1"] * near
 
     def third(row):
         near = beside(
-            p[row + 1, pl.ds(0, ny + 2)], p[row, pl.ds(1, ny)], p[row + 2, pl.ds(1, ny)]
+            p(row)[row + 1, pl.ds(0, ny + 2)],
+            p(row - 1)[row, pl.ds(1, ny)],
+            p(row + 1)[row + 2, pl.ds(1, ny)],
         )
-        own = p[row + 1, pl.ds(1, ny)]
-        begin = u[row + 3, pl.ds(3, ny)] + k["start2"] * q[row + 2, pl.ds(2, ny)]
+        own = p(row)[row + 1, pl.ds(1, ny)]
+        begin = u[row + 3, pl.ds(3, ny)] + k["start2"] * q(row)[row + 2, pl.ds(2, ny)]
         finish(row, (begin + w2[row][:, None] * own) + k["side2"] * near)
 
     for row in range(-2, nx + 6):
-        if row < nx + 2:
+        if row < nx + 2 and wanted(row, 1):
             start(row)
-        if -1 <= row - 2 < nx + 1:
+        if -1 <= row - 2 < nx + 1 and wanted(row - 2, 2):
             second(row - 2)
-        if 0 <= row - 4 < nx:
+        if 0 <= row - 4 < nx and wanted(row - 4, 3):
             third(row - 4)
 
 
@@ -213,13 +236,13 @@
 
     sources, guesses, shifts = take(4), take(4), take(4)
     blocks, link_inputs = take(3), take(3)
-    start_out, source_out, w0_out, w1_out, w2_out = take(5)
+    start_out, source_out, w0_out, w1_out, w2_out, q_out, p_out, middle_out = take(8)
     outs = [None] + take(3)
     U, S = [start_out] + take(2), [source_out] + take(2)
     D, H = take(3), take(4)
     W0, W1, W2 = [w0_out] + take(2), [w1_out] + take(2), [w2_out] + take(2)
-    Q, PD = [None] + take(2), [None] + take(2)
-    V, T, W = take(3)
+    Q, PD = [q_out] + take(2), [p_out] + take(2)
+    V, T, W, N = take(4)
     B, BT, C = take(3), take(3), take(3)
     K, DK, QK, PK = take(4)
     links = take(3)
@@ -227,8 +250,13 @@
     gz, gy = lax.axis_index("gz"), lax.axis_index("gy")
     k = coefficients()
 
+    side = lax.rem(gy, 2)
+
     def at(ox, oy):
-        return (lax.rem(gz + (ox % peers[0]), peers[0]), lax.rem(gy + (oy % peers[1]), peers[1]))
+        oy = oy % peers[1] if isinstance(oy, int) else oy + peers[1]
+        return (lax.rem(gz + (ox % peers[0]), peers[0]), lax.rem(gy + oy, peers[1]))
+
+    partner = at(0, 1 - 2 * side)
 
     barrier = pltpu.get_barrier_semaphore()
     company = partners(dims, peers)
@@ -242,15 +270,13 @@
         copy.start()
         return copy
 
-    gather = Gather(dims[LAST], peers)
-    last_x, last_y = dims[LAST]
-    own_cells = [(x, y) for x in range(last_x) for y in range(last_y)]
+    gather = Gather(peers)
     loads = [None] * LEVELS
-    loads[LAST] = [fetch(shifts[LAST], H[LAST])]
-    for x, y in own_cells:
-        slot = gather.slot[(x, y)]
-        loads[LAST].append(fetch(guesses[LAST].at[x, y], K.at[slot, 0]))
-        loads[LAST].append(fetch(sources[LAST].at[x, y], K.at[slot, 1]))
+    loads[LAST] = [
+        fetch(guesses[LAST].at[0, 0], K.at[gather.row[0], gy, 0]),
+        fetch(sources[LAST].at[0, 0], K.at[gather.row[0], gy, 1]),
+        fetch(shifts[LAST], H[LAST]),
+    ]
 
     def own(ref, level, reach):
         nx, ny = dims[level]
@@ -270,8 +296,7 @@
 
     for copy in loads[LAST]:
         copy.wait()
-    for x, y in own_cells:
-        DK[gather.slot[(x, y)]] = 6.0 + H[LAST][x, pl.ds(y, 1)]
+    DK[gather.row[0], gy] = 6.0 + H[LAST][0]
 
     pl.semaphore_wait(barrier, len(company))
 
@@ -302,13 +327,26 @@
             for ox, oy, source, target, size in messages
         ]
 
+    def share(row, column, whole, device):
+        cell = (row, column)
+        if whole:
+            return [
+                send(K.at[cell], K.at[cell], device),
+                send(DK.at[cell], DK.at[cell], device),
+            ]
+        return [send(K.at[cell].at[0], K.at[cell].at[0], device)]
+
     last = []
-    for ox, oy, source, target, whole in gather.messages():
+    for x, y, whole in gather.messages():
+        source, target = (gather.row[0], gy), (gather.row[x], gy)
+        copies = []
         if whole:
-            last.append(send(K.at[source], K.at[target], at(ox, oy)))
-            last.append(send(DK.at[source], DK.at[target], at(ox, oy)))
+            copies.append(send(K.at[source], K.at[target], at(-x, -y)))
+            copies.append(send(DK.at[source], DK.at[target], at(-x, -y)))
         else:
-            last.append(send(K.at[source, 0], K.at[target, 0], at(ox, oy)))
+            copies.append(send(K.at[source].at[0], K.at[target].at[0], at(-x, -y)))
+        last.append((gather.row[x], lax.rem(gy + y, peers[1]), whole, copies))
+    handed = share(gather.row[0], gy, True, partner)
 
     def diagonals(level):
         nx, ny = dims[level]
@@ -344,13 +382,18 @@
         block_loads[level].wait()
         line = B[level].shape[-1]
 
-        def body(cell, carry):
-            i, j = cell // ny, cell % ny
-            for side in range(2):
-                BT[level][i, j, pl.ds(side * line, line)] = B[level][i, j, side].T
+        def body(i, carry):
+            for j in range(ny):
+                for part in range(2):
+                    BT[level][i, j, pl.ds(part * line, line)] = B[level][i, j, part].T
             return carry
 
-        lax.fori_loop(0, nx * ny, body, 0)
+        lax.fori_loop(0, nx, body, 0)
+
+    def relax(level, finish, middle=None):
+        weights = W0[level], W1[level], W2[level]
+        q, p = Q[level], PD[level]
+        smoothing(*dims[level], U[level], S[level], *weights, lambda r: q, lambda r: p, finish, middle)
 
     def smooth(level):
         nx, ny = dims[level]
@@ -360,37 +403,81 @@
             lines = result.reshape(result.shape[:1] + C[level - 1].shape[2:])
             C[level - 1][row + 1, pl.ds(1, ny)] = lines.astype(jnp.bfloat16)
 
-        smoothing(
-            nx, ny, U[level], S[level], W0[level], W1[level], W2[level], Q[level], PD[level], finish
-        )
+        relax(level, finish)
 
     def smooth_last():
+        column = [lax.rem(gy + y, peers[1]) for y in range(peers[1])]
+
+        def place(x, y):
+            return gather.row[x % peers[0]], column[y % peers[1]]
+
         def near(ref, x, y):
-            def cell(a, b):
-                return ref[gather.slot[gather.at(a, b)]]
-
-            middle = cell(x, y)
-            total = (cell(x, y - 1) + cell(x, y + 1)) + (cell(x - 1, y) + cell(x + 1, y))
+            middle = ref[place(x, y)]
+            total = ref[place(x, y - 1)] + ref[place(x, y + 1)]
+            total = total + (ref[place(x - 1, y)] + ref[place(x + 1, y)])
             line = middle.shape[-1]
             return middle, total + (pltpu.roll(middle, 1, 2) + pltpu.roll(middle, line - 1, 2))
 
         for x, y in gather.around(2):
-            slot = gather.slot[(x, y)]
-            middle, total = near(K.at[:, 0], x, y)
-            QK[slot] = (K[slot, 1] - DK[slot] * middle) + total
+            middle, total = near(K.at[:, :, 0], x, y)
+            QK[place(x, y)] = (K[place(x, y) + (1,)] - DK[place(x, y)] * middle) + total
         for x, y in gather.around(1):
-            slot = gather.slot[(x, y)]
             middle, total = near(QK, x, y)
-            PK[slot] = (k["own1"] - k["side1"] * DK[slot]) * middle + k["side1"] * total
-        for x in range(-1, last_x + 1):
-            for y in range(-1, last_y + 1):
-                slot = gather.slot[gather.at(x, y)]
+            weight = k["own1"] - k["side1"] * DK[place(x, y)]
+            PK[place(x, y)] = weight * middle + k["side1"] * total
+        for x in range(-1, 2):
+            for y in range(-1, 2):
                 middle, total = near(PK, x, y)
-                begin = K[slot, 0] + k["start2"] * QK[slot]
-                result = begin + (k["own2"] - k["side2"] * DK[slot]) * middle + k["side2"] * total
-                if (x, y) in own_cells:
-                    outs[LAST][x, y] = result
+                weight = k["own2"] - k["side2"] * DK[place(x, y)]
+                begin = K[place(x, y) + (0,)] + k["start2"] * QK[place(x, y)]
+                result = begin + weight * middle + k["side2"] * total
+                if x == 0 and y == 0:
+                    outs[LAST][0, 0] = result
                 C[LAST - 1][x + 1, y + 1] = result.reshape(C[LAST - 1].shape[2:]).astype(jnp.bfloat16)
+
+    outer = []
+
+    def begin(level):
+        nx, ny = dims[level]
+        u = U[level]
+        near, rest = straight(nx, ny)
+        first = list(zip(near, exchange(u, REACH, near)))
+        later = []
+        for ox, target, source, width in corners(nx, ny):
+            start = side * (ny - width) + REACH
+            stop = side * (-width - ny) + ny + REACH
+            later.append(
+                send(
+                    u.at[source + REACH, pl.ds(start, width)],
+                    u.at[target + REACH, pl.ds(stop, width)],
+                    at(ox, 2 * side - 1),
+                )
+            )
+        if level == 1:
+            for slot, ox in enumerate((1, -1)):
+                outer.append(send(N.at[slot], N.at[slot + 2], at(ox, 0)))
+            rest = [m for m in rest if not m[0]]
+        later += exchange(u, REACH, rest)
+        return first, later
+
+    def pass_on(level, first):
+        nx, ny = dims[level]
+        u = U[level]
+        widths = {target: width for _, target, _, width in corners(nx, ny)}
+        copies = []
+        for m, copy in first:
+            copy.wait_recv()
+            row, width = m[3][0], widths[m[3][0]]
+            start = (1 - side) * (ny - width) + REACH
+            stop = (1 - side) * (-width - ny) + ny + REACH
+            copies.append(
+                send(
+                    u.at[row + REACH, pl.ds(start, width)],
+                    u.at[row + REACH, pl.ds(stop, width)],
+                    partner,
+                )
+            )
+        return copies
 
     def prolong(level, rows):
         nx, ny = dims[level]
@@ -423,6 +510,10 @@
                         W[0, j] = sums.astype(jnp.bfloat16)
                     if i == nx - 1:
                         W[1, j] = sums.astype(jnp.bfloat16)
+                if level == 1:
+                    for slot, row in enumerate((nx - REACH, REACH - 1)):
+                        if i == row:
+                            N[slot, j] = u.reshape(sums.shape).astype(jnp.bfloat16)
 
     def widen(source, target, pad, corner, size):
         for row in range(corner[0] + pad, corner[0] + pad + size[0]):
@@ -433,6 +524,7 @@
     diagonals(2)
     side2 = sides(2)
     diagonals(1)
+    side1 = sides(1)
     diagonals(0)
     nx, ny = dims[0]
     for i in range(nx):
@@ -445,14 +537,17 @@
         for copy in copies:
             copy.wait_recv()
 
-    wait(last)
+    for row, column, whole, copies in last:
+        wait(copies)
+        handed += share(row, column, whole, partner)
+    wait(handed)
     smooth_last()
     prolong(2, range(dims[2][0]))
-    begin2 = exchange(U[2], REACH, plan(*dims[2], REACH))
-    side1 = sides(1)
+    first2, later2 = begin(2)
     wait(side2)
     weigh(2)
-    wait(begin2)
+    handed2 = pass_on(2, first2)
+    wait(later2 + handed2)
     smooth(2)
     coarse1 = exchange(C[1], 1, plan(*dims[2], 1, True))
     side0 = sides(0, T)
@@ -460,14 +555,21 @@
     weigh(1)
     wait(coarse1)
     prolong(1, range(dims[1][0]))
-    begin1 = exchange(U[1], REACH, plan(*dims[1], REACH))
+    first1, later1 = begin(1)
     messages = plan(*dims[0], REACH - 1)
     wait(side0)
     for m in messages:
         if m[0]:
             widen(T, S[0], 2, m[3], m[4])
     weigh(0)
-    wait(begin1)
+    handed1 = pass_on(1, first1)
+    for slot, copy in enumerate(outer):
+        copy.wait_recv()
+        row = (0, dims[1][0] + 2 * REACH - 1)[slot]
+        value = N[slot + 2].astype(jnp.float32)
+        cells = pl.ds(REACH, dims[1][1])
+        U[1][row, cells] = value.reshape(value.shape[:1] + U[1].shape[2:])
+    wait(later1 + handed1)
     smooth(1)
     coarse0 = exchange(C[0], 1, plan(*dims[1], 1, True))
     edges = ((1, nx - 1, -1, 1, 2), (-1, 0, nx, 0, 3))
@@ -480,18 +582,29 @@
     for copy in early:
         copy.wait_send()
 
+    third = range(min(REACH, nx)), range(max(nx - REACH, 0), nx), range(nx)
+    segments = []
+    for rows in third:
+        segments.append([i for i in rows if not any(i in segment for segment in segments)])
     messages = []
     for ox, oy, source, target, size in plan(*dims[0], REACH):
         if ox and not oy:
             shift = 1 if ox < 0 else 0
             source, target = (source[0] + shift, source[1]), (target[0] + shift, target[1])
-            size = (size[0] - 1, size[1])
-        messages.append((ox, oy, source, target, size))
+            messages.append((ox, oy, source, target, (size[0] - 1, size[1]), V))
+        elif ox:
+            messages.append((ox, oy, source, target, size, V))
+        else:
+            for segment in segments:
+                for col in range(size[1]):
+                    near = beyond(target[1] + col, ny) == 1
+                    place = (segment[0], source[1] + col), (segment[0], target[1] + col)
+                    messages.append((0, oy) + place + ((len(segment), 1), U[0] if near else V))
+    sent = len(pending)
     begin0 = []
     slim = []
     done = set()
-    for rows in (range(min(REACH, nx)), range(max(nx - REACH, 0), nx), range(nx)):
-        fresh = [i for i in rows if i not in done]
+    for fresh in segments:
         done.update(fresh)
         prolong(0, fresh)
         for ox, row, place, slot, landing in edges:
@@ -500,7 +613,19 @@
         ready = [m for m in messages if all(m[2][0] + i in done for i in range(m[4][0]))]
         messages = [m for m in messages if m not in ready]
         for m in ready:
-            begin0.append((m, exchange(V if m[0] else U[0], REACH, [m])[0]))
+            begin0.append((m, exchange(m[5], REACH, [m[:5]])[0]))
+    for copy in pending[:sent]:
+        copy.wait_send()
+    for m, copy in begin0:
+        if not m[0]:
+            copy.wait_recv()
+            if m[5] is V:
+                widen(V, U[0], REACH, m[3], m[4])
+
+    def finish(row, result):
+        middle_out[row] = result
+
+    relax(0, finish, True)
     wait(early)
     for place, landing, copy in slim:
         copy.wait_recv()
@@ -508,17 +633,17 @@
         guess = U[0][place + REACH, pl.ds(REACH, ny)]
         U[0][place + REACH, pl.ds(REACH, ny)] = guess + value.reshape(guess.shape)
     for m, copy in begin0:
-        copy.wait_recv()
         if m[0]:
+            copy.wait_recv()
             widen(V, U[0], REACH, m[3], m[4])
-    for copy in pending:
+    for copy in pending[sent:]:
         copy.wait_send()
 
 
 def finishing(nx, ny, *refs):
-    u, s, w0, w1, w2 = refs[:5]
-    values, outs = refs[5:8], refs[8:12]
-    q, p, o, sem = refs[12:]
+    u, s, w0, w1, w2, q_held, p_held, middle = refs[:8]
+    values, outs = refs[8:11], refs[11:15]
+    q, p, o, sem = refs[15:]
     copies = []
 
     def store(source, target):
@@ -528,12 +653,17 @@
 
     for value, out in zip(values, outs[1:]):
         store(value, out)
+    for row in range(3, nx - 3):
+        store(middle.at[row], outs[0].at[row])
 
     def finish(row, result):
         o[row] = result
         store(o.at[row], outs[0].at[row])
 
-    smoothing(nx, ny, u, s, w0, w1, w2, q, p, finish)
+    def rows(held, fresh, margin):
+        return lambda row: held if margin <= row < nx - margin else fresh
+
+    smoothing(nx, ny, u, s, w0, w1, w2, rows(q_held, q, 1), rows(p_held, p, 2), finish, False)
     for copy in copies:
         copy.wait()
 
@@ -562,8 +692,11 @@
         grown(0, 4, tile),
         grown(0, 2, tile),
         grown(0, 0, tile),
+        grown(0, 4, line),
+        grown(0, 2, line),
+        grown(0, 0, line),
     ] + [grown(level, 0, line) for level in (1, 2, 3)]
-    slots = len(Gather(dims[LAST], peers).u)
+    kept = (len(Gather(peers).row), peers[1])
     scratch = (
         [grown(n, 2 * REACH, line) for n in middle]
         + [grown(n, 4, line) for n in middle]
@@ -575,15 +708,15 @@
         + [grown(n, 4, line) for n in middle]
         + [grown(n, 2, line) for n in middle]
         + [grown(0, 2 * REACH, packed, jnp.bfloat16), grown(0, 4, packed, jnp.bfloat16)]
-        + [((4, dims[0][1]) + packed, jnp.bfloat16)]
+        + [((4, dims[n][1]) + packed, jnp.bfloat16) for n in (0, 1)]
         + [(x.shape, x.dtype) for x in args[12:15]]
         + [(x.shape[:2] + (2 * width, width), x.dtype) for x in args[12:15]]
         + [grown(n, 2, packed, jnp.bfloat16) for n in range(1, LEVELS)]
         + [
-            ((slots, 2) + line, jnp.float32),
-            ((slots, 1, width), jnp.float32),
-            ((slots,) + line, jnp.float32),
-            ((slots,) + line, jnp.float32),
+            (kept + (2,) + line, jnp.float32),
+            (kept + (1, width), jnp.float32),
+            (kept + line, jnp.float32),
+            (kept + line, jnp.float32),
         ]
     )
     messages = message_count(dims, peers)

time: 57.7 us -> 52.8 us (0.915)
  Pallas kernels: 56.9 us -> 52 us
    pallas_call x1, Pallas kernels: 54.6 us -> 50.4 us  [shards(): pl.pallas_call(partial(upward, dims, peers), out_shape=[pltpu.VMEM(*r) fo...]
    pallas_call x1, Pallas kernels: 2.24 us -> 1.58 us  [shards(): pl.pallas_call(partial(finishing, nx, ny), out_shape=[jax.ShapeDtypeStruc...]
where the time goes in v2:
time: 52.8 us; the launch traced here: 52.6 us
  Pallas kernels  52 us (98%)
  between operations  0.65 us (1%)
    pallas_call x1, Pallas kernels, shards(): pl.pallas_call(partial(upward, dims, peers), out_shape=[pltpu.VMEM(*r) fo...  50.4 us
    pallas_call x1, Pallas kernels, shards(): pl.pallas_call(partial(finishing, nx, ny), out_shape=[jax.ShapeDtypeStruc...  1.58 us

profile of v2, /device:TPU:0, one launch (start us, length us, event | category | flops | bytes accessed | tf_op | source)
XLA Modules:
  0.0 52.6 jit_solution(4105359769944032317)
XLA Ops:
  0.6 50.4 %shard_map.201 = (f32[14,14,2,8,128]{4,3,2,1,0:T(8,128)S(1)}, f32[12,12,2,8,128]{4,3,2,1,0:T(8,128)S(1)}, f32[12,12,8,128]{3,2,1,0:T(8,128)S(1)}, f32[10,10,8,12...) custom-call(f32[8,8,2,8,128]{4,3,2,1,0:T(8,128)} %bitcast.14, ...), custom_call_target="tpu_custom_call" | custom-call | tf_op jit(solution)/shard_map/pallas_call | solution.py:725
  51.0 1.6 %shard_map.202 = (f32[8,8,2,8,128]{4,3,2,1,0:T(8,128)}, f32[4,4,2,8,128]{4,3,2,1,0:T(8,128)}, f32[2,2,2,8,128]{4,3,2,1,0:T(8,128)}, f32[1,1,2,8,128]{4,3,2,1,0:T(8,128)}) custom-call(f32[14,14,2,8,128]{4,3,2,1,0:T(8,128)S(1)} %get-tuple-element.19.refs_0_, f32[12,12,2,8,128]{4,3,2,1,0:T(8,128)S(1)} %get-tuple-element.20.refs_1_, ...), custom_call_target="tpu_custom_call" | custom-call | tf_op jit(solution)/shard_map/pallas_call | solution.py:742

commit v3 on v2

--- a/solution.py
+++ b/solution.py
@@ -143,9 +143,23 @@
     return near, rest
 
 
+def slab(nx, reach, peers):
+    far = -(-reach // nx)
+    out = []
+    for ox in range(-far, far + 1):
+        for oy in range(0, peers[1], 2):
+            top, end = max(-ox * nx, -reach), min((1 - ox) * nx, nx + reach)
+            if (ox or oy) and top < end:
+                out.append((ox, oy, top + ox * nx, top, end - top))
+    out.sort(key=lambda m: (abs(m[0]) + min(m[1], peers[1] - m[1]), m))
+    return out
+
+
 def message_count(dims, peers):
-    total = 6 + 2 * sum(1 + m[-1] for m in Gather(peers).messages())
-    for level, (nx, ny) in enumerate(dims[:LAST]):
+    total = 14 + 2 * sum(1 + m[-1] for m in Gather(peers).messages())
+    third = dims[LAST - 1][0]
+    total += 2 * (1 + len(slab(third, REACH + 1, peers)) + 2 * len(slab(third, REACH, peers)) + 2)
+    for level, (nx, ny) in enumerate(dims[: LAST - 1]):
         total += len(plan(nx, ny, REACH)) + 2 * len(plan(nx, ny, REACH - 1))
         if level:
             total += len(plan(nx, ny, 1, True)) + 4 * REACH
@@ -156,12 +170,13 @@
 
 def partners(dims, peers):
     found = set()
-    for nx, ny in dims[:LAST]:
+    for nx, ny in dims[: LAST - 1]:
         for m in plan(nx, ny, REACH) + plan(nx, ny, 1, True):
             found.add((m[0] % peers[0], m[1] % peers[1]))
             found.add((-m[0] % peers[0], -m[1] % peers[1]))
-    for x, y, _ in Gather(peers).messages():
-        found.add((x, y))
+    around = [m[:2] for m in slab(dims[LAST - 1][0], REACH + 1, peers)]
+    for x, y in around + [m[:2] for m in Gather(peers).messages()]:
+        found.add((x % peers[0], y % peers[1]))
         found.add((-x % peers[0], -y % peers[1]))
     return sorted(found)
 
@@ -173,57 +188,74 @@
 def beside(centre, above, below):
     middle = centre[1:-1]
     line = middle.shape[-1]
-    total = (centre[:-2] + centre[2:]) + (above + below)
+    total = centre[:-2] + centre[2:]
+    for other in (above, below):
+        if other is not None:
+            total = total + other
     return total + (pltpu.roll(middle, 1, 3) + pltpu.roll(middle, line - 1, 3))
 
 
-def smoothing(nx, ny, u, s, w0, w1, w2, q, p, finish, middle=None):
+def smoothing(nx, ny, u, s, w0, w1, w2, q, p, finish, middle=None, held=None):
     k = coefficients()
 
-    def wanted(row, margin):
-        return middle is None or (margin <= row < nx - margin) == middle
-
-    def start(row):
+    def share(row, margin):
+        if middle is None:
+            return "all"
+        inside = margin <= row < nx - margin
+        edge = row in (margin - 1, nx - margin) and nx > 2 * REACH
+        if middle:
+            return "all" if inside else "inner" if edge else None
+        return None if inside else "outer" if edge else "all"
+
+    def around(ref, row, pad, cells, part, margin):
+        sides = []
+        for other in (row - 1, row + 1):
+            outer = (other < row) == (row == margin - 1)
+            wanted = part == "all" or (part == "outer") == outer
+            sides.append(ref(other)[other + pad, cells] if wanted else None)
+        return [x for x in sides if x is not None][0] if part == "outer" else sides
+
+    def start(row, part):
         w = 2 - beyond(row, nx)
         count = ny + 2 * w
-        near = beside(
-            u[row + 3, pl.ds(2 - w, count + 2)],
-            u[row + 2, pl.ds(3 - w, count)],
-            u[row + 4, pl.ds(3 - w, count)],
-        )
-        own = u[row + 3, pl.ds(3 - w, count)]
-        weight = w0[row + 2, pl.ds(2 - w, count)][:, None]
-        q(row)[row + 2, pl.ds(2 - w, count)] = (s[row + 2, pl.ds(2 - w, count)] - weight * own) + near
-
-    def second(row):
+        cells, inner = pl.ds(2 - w, count), pl.ds(3 - w, count)
+        others = around(lambda _: u, row, 3, inner, part, 1)
+        if part == "outer":
+            q(row)[row + 2, cells] = held[0][row + 2, cells] + others
+            return
+        near = beside(u[row + 3, pl.ds(2 - w, count + 2)], *others)
+        weight = w0[row + 2, cells][:, None]
+        q(row)[row + 2, cells] = (s[row + 2, cells] - weight * u[row + 3, inner]) + near
+
+    def second(row, part):
         w = 1 - beyond(row, nx)
         count = ny + 2 * w
-        near = beside(
-            q(row)[row + 2, pl.ds(1 - w, count + 2)],
-            q(row - 1)[row + 1, pl.ds(2 - w, count)],
-            q(row + 1)[row + 3, pl.ds(2 - w, count)],
-        )
-        own = q(row)[row + 2, pl.ds(2 - w, count)]
-        weight = w1[row + 1, pl.ds(1 - w, count)][:, None]
-        p(row)[row + 1, pl.ds(1 - w, count)] = weight * own + k["side1"] * near
-
-    def third(row):
-        near = beside(
-            p(row)[row + 1, pl.ds(0, ny + 2)],
-            p(row - 1)[row, pl.ds(1, ny)],
-            p(row + 1)[row + 2, pl.ds(1, ny)],
-        )
-        own = p(row)[row + 1, pl.ds(1, ny)]
+        cells, inner = pl.ds(1 - w, count), pl.ds(2 - w, count)
+        others = around(q, row, 2, inner, part, 2)
+        if part == "outer":
+            p(row)[row + 1, cells] = held[1][row + 1, cells] + k["side1"] * others
+            return
+        near = beside(q(row)[row + 2, pl.ds(1 - w, count + 2)], *others)
+        weight = w1[row + 1, cells][:, None]
+        p(row)[row + 1, cells] = weight * q(row)[row + 2, inner] + k["side1"] * near
+
+    def third(row, part):
+        cells = pl.ds(1, ny)
+        others = around(p, row, 1, cells, part, 3)
+        if part == "outer":
+            finish(row, held[2][row] + k["side2"] * others)
+            return
+        near = beside(p(row)[row + 1, pl.ds(0, ny + 2)], *others)
         begin = u[row + 3, pl.ds(3, ny)] + k["start2"] * q(row)[row + 2, pl.ds(2, ny)]
-        finish(row, (begin + w2[row][:, None] * own) + k["side2"] * near)
+        finish(row, (begin + w2[row][:, None] * p(row)[row + 1, cells]) + k["side2"] * near)
 
     for row in range(-2, nx + 6):
-        if row < nx + 2 and wanted(row, 1):
-            start(row)
-        if -1 <= row - 2 < nx + 1 and wanted(row - 2, 2):
-            second(row - 2)
-        if 0 <= row - 4 < nx and wanted(row - 4, 3):
-            third(row - 4)
+        if row < nx + 2 and share(row, 1):
+            start(row, share(row, 1))
+        if -1 <= row - 2 < nx + 1 and share(row - 2, 2):
+            second(row - 2, share(row - 2, 2))
+        if 0 <= row - 4 < nx and share(row - 4, 3):
+            third(row - 4, share(row - 4, 3))
 
 
 def upward(dims, peers, *refs):
@@ -242,9 +274,10 @@
     D, H = take(3), take(4)
     W0, W1, W2 = [w0_out] + take(2), [w1_out] + take(2), [w2_out] + take(2)
     Q, PD = [q_out] + take(2), [p_out] + take(2)
-    V, T, W, N = take(4)
+    V, T, W, N, M = take(5)
     B, BT, C = take(3), take(3), take(3)
     K, DK, QK, PK = take(4)
+    R = refs.pop(0)
     links = take(3)
     local_sem, send_sem, recv_sem = take(3)
     gz, gy = lax.axis_index("gz"), lax.axis_index("gy")
@@ -282,12 +315,17 @@
         nx, ny = dims[level]
         return ref.at[pl.ds(reach, nx), pl.ds(reach, ny)]
 
+    third = LAST - 1
+    mine = pl.ds(gy * dims[third][1], dims[third][1])
     for level in reversed(range(LAST)):
-        loads[level] = [
-            fetch(shifts[level], H[level]),
-            fetch(sources[level], own(S[level], level, REACH - 1)),
-            fetch(guesses[level], own(U[level], level, REACH)),
-        ]
+        loads[level] = [fetch(shifts[level], H[level])]
+        if level == third:
+            rows = dims[third][0]
+            loads[level].append(fetch(sources[level], S[level].at[pl.ds(REACH, rows), mine]))
+            loads[level].append(fetch(guesses[level], U[level].at[pl.ds(REACH + 1, rows), mine]))
+        else:
+            loads[level].append(fetch(sources[level], own(S[level], level, REACH - 1)))
+            loads[level].append(fetch(guesses[level], own(U[level], level, REACH)))
     for level in reversed(range(LAST)):
         loads[level].append(fetch(link_inputs[level], links[level]))
     block_loads = [None] * LAST
@@ -354,7 +392,11 @@
             copy.wait()
         for i in range(nx):
             for j in range(ny):
-                D[level][i + 2, j + 2] = 6.0 + H[level][i, pl.ds(j, 1)]
+                d = 6.0 + H[level][i, pl.ds(j, 1)]
+                if level == third:
+                    D[level][i + REACH, gy * ny + j] = d
+                else:
+                    D[level][i + 2, j + 2] = d
 
     def sides(level, narrow=None):
         messages = plan(*dims[level], REACH - 1)
@@ -363,6 +405,41 @@
             ref = S[level] if narrow is None or m[0] == 0 else narrow
             copies += exchange(ref, 2, [m])
         return copies + exchange(D[level], 2, messages)
+
+    def sides_second():
+        nx, ny = dims[1]
+        s = S[1]
+        copies, near, thin = [], [], []
+        for slot, row in enumerate((nx - 2, 1)):
+            value = s[row + 2, pl.ds(2, ny)]
+            M[slot] = value.reshape(value.shape[:1] + M.shape[2:]).astype(jnp.bfloat16)
+        for slot, (ox, source, target) in enumerate(((1, nx - 1, -1), (-1, 0, nx))):
+            cells = pl.ds(2, ny)
+            near.append((target, send(s.at[source + 2, cells], s.at[target + 2, cells], at(ox, 0))))
+            start, stop = side * (ny - 1) + 2, side * (-1 - ny) + ny + 2
+            corner = s.at[source + 2, pl.ds(start, 1)], s.at[target + 2, pl.ds(stop, 1)]
+            copies.append(send(*corner, at(ox, 2 * side - 1)))
+            thin.append(send(M.at[slot], M.at[slot + 2], at(ox, 0)))
+        messages = plan(nx, ny, REACH - 1)
+        copies += exchange(s, 2, [m for m in messages if not m[0]])
+        return copies + exchange(D[1], 2, messages), near, thin
+
+    def finish_second(copies, near, thin):
+        nx, ny = dims[1]
+        s = S[1]
+        handed = []
+        for target, copy in near:
+            copy.wait_recv()
+            start = (1 - side) * (ny - 1) + 2
+            stop = (1 - side) * (-1 - ny) + ny + 2
+            corner = s.at[target + 2, pl.ds(start, 1)], s.at[target + 2, pl.ds(stop, 1)]
+            handed.append(send(*corner, partner))
+        for slot, copy in enumerate(thin):
+            copy.wait_recv()
+            value = M[slot + 2].astype(jnp.float32)
+            row = (0, nx + 3)[slot]
+            s[row, pl.ds(2, ny)] = value.reshape(value.shape[:1] + s.shape[2:])
+        wait(copies + handed)
 
     def weigh(level):
         nx, ny = dims[level]
@@ -376,6 +453,59 @@
                     W1[level][row + 1, col + 1] = k["own1"] - k["side1"] * d
                 if far == 0:
                     W2[level][row, col] = k["own2"] - k["side2"] * d
+
+    def spread(ref, reach):
+        nx = dims[third][0]
+        whole = pl.ds(reach, nx)
+        copies = []
+        for ox, oy, source, target, count in slab(nx, REACH + 1 if ref is U[third] else REACH, peers):
+            start, stop = pl.ds(source + reach, count), pl.ds(target + reach, count)
+            column = lax.rem(gy + peers[1] - oy, peers[1]) * dims[third][1]
+            copy = send(ref.at[start, mine], ref.at[stop, mine], at(ox, oy))
+            copies.append((stop, pl.ds(column, dims[third][1]), copy))
+        return copies, [send(ref.at[whole, mine], ref.at[whole, mine], partner)]
+
+    def hand(ref, copies, handed):
+        for rows, columns, copy in copies:
+            copy.wait_recv()
+            handed.append(send(ref.at[rows, columns], ref.at[rows, columns], partner))
+
+    def weigh_third():
+        nx, columns = dims[third][0], D[third].shape[1]
+        for row in range(-REACH, nx + REACH):
+            for col in range(columns):
+                d = jnp.broadcast_to(D[third][row + REACH, col], W0[third].shape[2:])
+                W0[third][row + REACH, col] = d
+                if -2 <= row < nx + 2:
+                    W1[third][row + 2, col] = k["own1"] - k["side1"] * d
+                if -1 <= row < nx + 1:
+                    W2[third][row + 1, col] = k["own2"] - k["side2"] * d
+
+    def smooth_third():
+        nx, ny = dims[third]
+        u, s, q, p = U[third], S[third], Q[third], PD[third]
+
+        def near(ref, row):
+            middle = ref[row]
+            ring = jnp.concatenate([middle[-1:], middle, middle[:1]], axis=0)
+            return middle, beside(ring, ref[row - 1], ref[row + 1])
+
+        for row in range(-3, nx + 3):
+            middle, total = near(u, row + 4)
+            q[row + 3] = (s[row + 3] - W0[third][row + 3][:, None] * middle) + total
+        for row in range(-2, nx + 2):
+            middle, total = near(q, row + 3)
+            p[row + 2] = W1[third][row + 2][:, None] * middle + k["side1"] * total
+        for row in range(-1, nx + 1):
+            middle, total = near(p, row + 2)
+            begin = u[row + 4] + k["start2"] * q[row + 3]
+            result = begin + W2[third][row + 1][:, None] * middle + k["side2"] * total
+            lines = result.reshape(result.shape[:1] + C[third - 1].shape[2:])
+            C[third - 1][row + 1] = lines.astype(jnp.bfloat16)
+            if 0 <= row < nx:
+                R[row] = result
+        for row in range(nx):
+            outs[third][row] = R[row, mine]
 
     def turn(level):
         nx, ny = dims[level]
@@ -492,8 +622,10 @@
             else:
                 link = links[level][i, j, side]
             row = modulo(quotient(link, full[1]) + lift_x, full[0])
-            col = modulo(modulo(link, full[1]) + lift_y, full[1])
-            return C[level][jnp.minimum(row, cx + 1), jnp.minimum(col, cy + 1)]
+            col = modulo(link, full[1])
+            if level + 1 != third:
+                col = jnp.minimum(modulo(col + lift_y, full[1]), cy + 1)
+            return C[level][jnp.minimum(row, cx + 1), col]
 
         for i in rows:
             for j in range(ny):
@@ -501,9 +633,12 @@
                 sums = lax.dot_general(
                     picked, BT[level][i, j], (((1,), (0,)), ((), ())), preferred_element_type=jnp.float32
                 )
-                u = U[level][i + REACH, j + REACH]
+                place = i + REACH, j + REACH
+                if level == third:
+                    place = i + REACH + 1, gy * ny + j
+                u = U[level][place]
                 u = u + sums.reshape(u.shape)
-                U[level][i + REACH, j + REACH] = u
+                U[level][place] = u
                 if level == 0:
                     V[i + REACH, j + REACH] = u.reshape(sums.shape).astype(jnp.bfloat16)
                     if i == 0:
@@ -522,9 +657,8 @@
             target[row, cells] = value.reshape(value.shape[:1] + target.shape[2:])
 
     diagonals(2)
-    side2 = sides(2)
+    side2 = spread(S[third], REACH), spread(D[third], REACH)
     diagonals(1)
-    side1 = sides(1)
     diagonals(0)
     nx, ny = dims[0]
     for i in range(nx):
@@ -543,25 +677,21 @@
     wait(handed)
     smooth_last()
     prolong(2, range(dims[2][0]))
-    first2, later2 = begin(2)
-    wait(side2)
-    weigh(2)
-    handed2 = pass_on(2, first2)
-    wait(later2 + handed2)
-    smooth(2)
-    coarse1 = exchange(C[1], 1, plan(*dims[2], 1, True))
+    first2, later2 = spread(U[third], REACH + 1)
+    side1 = sides_second()
     side0 = sides(0, T)
-    wait(side1)
-    weigh(1)
-    wait(coarse1)
+    for ref, (copies, handed) in zip((S[third], D[third]), side2):
+        hand(ref, copies, handed)
+    hand(U[third], first2, later2)
+    for _, handed in side2:
+        wait(handed)
+    weigh_third()
+    wait(later2)
+    smooth_third()
     prolong(1, range(dims[1][0]))
     first1, later1 = begin(1)
-    messages = plan(*dims[0], REACH - 1)
-    wait(side0)
-    for m in messages:
-        if m[0]:
-            widen(T, S[0], 2, m[3], m[4])
-    weigh(0)
+    finish_second(*side1)
+    weigh(1)
     handed1 = pass_on(1, first1)
     for slot, copy in enumerate(outer):
         copy.wait_recv()
@@ -614,6 +744,12 @@
         messages = [m for m in messages if m not in ready]
         for m in ready:
             begin0.append((m, exchange(m[5], REACH, [m[:5]])[0]))
+    outline = plan(*dims[0], REACH - 1)
+    wait(side0)
+    for m in outline:
+        if m[0]:
+            widen(T, S[0], 2, m[3], m[4])
+    weigh(0)
     for copy in pending[:sent]:
         copy.wait_send()
     for m, copy in begin0:
@@ -663,7 +799,9 @@
     def rows(held, fresh, margin):
         return lambda row: held if margin <= row < nx - margin else fresh
 
-    smoothing(nx, ny, u, s, w0, w1, w2, rows(q_held, q, 1), rows(p_held, p, 2), finish, False)
+    q_rows, p_rows = rows(q_held, q, 1), rows(p_held, p, 2)
+    held = q_held, p_held, middle
+    smoothing(nx, ny, u, s, w0, w1, w2, q_rows, p_rows, finish, False, held)
     for copy in copies:
         copy.wait()
 
@@ -685,7 +823,12 @@
         nx, ny = dims[level]
         return (nx + extra, ny + extra) + shape, dtype
 
-    middle = (1, 2)
+    third = dims[LAST - 1]
+    columns = third[1] * peers[1]
+
+    def rows(extra, shape, dtype=jnp.float32):
+        return (third[0] + extra, columns) + shape, dtype
+
     results = [
         grown(0, 2 * REACH, line),
         grown(0, 4, line),
@@ -698,25 +841,30 @@
     ] + [grown(level, 0, line) for level in (1, 2, 3)]
     kept = (len(Gather(peers).row), peers[1])
     scratch = (
-        [grown(n, 2 * REACH, line) for n in middle]
-        + [grown(n, 4, line) for n in middle]
-        + [grown(n, 4, (1, width)) for n in range(LAST)]
+        [grown(1, 2 * REACH, line), rows(8, line)]
+        + [grown(1, 4, line), rows(6, line)]
+        + [grown(0, 4, (1, width)), grown(1, 4, (1, width)), rows(6, (1, width))]
         + [grown(n, 0, (width,)) for n in range(LEVELS)]
-        + [grown(n, 4, tile) for n in middle]
-        + [grown(n, 2, tile) for n in middle]
-        + [grown(n, 0, tile) for n in middle]
-        + [grown(n, 4, line) for n in middle]
-        + [grown(n, 2, line) for n in middle]
+        + [grown(1, 4, tile), rows(6, tile)]
+        + [grown(1, 2, tile), rows(4, tile)]
+        + [grown(1, 0, tile), rows(2, tile)]
+        + [grown(1, 4, line), rows(6, line)]
+        + [grown(1, 2, line), rows(4, line)]
         + [grown(0, 2 * REACH, packed, jnp.bfloat16), grown(0, 4, packed, jnp.bfloat16)]
-        + [((4, dims[n][1]) + packed, jnp.bfloat16) for n in (0, 1)]
+        + [((4, dims[n][1]) + packed, jnp.bfloat16) for n in (0, 1, 1)]
         + [(x.shape, x.dtype) for x in args[12:15]]
         + [(x.shape[:2] + (2 * width, width), x.dtype) for x in args[12:15]]
-        + [grown(n, 2, packed, jnp.bfloat16) for n in range(1, LEVELS)]
+        + [
+            grown(1, 2, packed, jnp.bfloat16),
+            rows(2, packed, jnp.bfloat16),
+            grown(LAST, 2, packed, jnp.bfloat16),
+        ]
         + [
             (kept + (2,) + line, jnp.float32),
             (kept + (1, width), jnp.float32),
             (kept + line, jnp.float32),
             (kept + line, jnp.float32),
+            rows(0, line),
         ]
     )
     messages = message_count(dims, peers)

time: 52.8 us -> 50.9 us (0.964)
  Pallas kernels: 52 us -> 50.1 us
    pallas_call x1, Pallas kernels: 50.4 us -> 48.7 us  [shards(): pl.pallas_call(partial(upward, dims, peers), out_shape=[pltpu.VMEM(*r) fo...]
where the time goes in v3:
time: 50.9 us; the launch traced here: 50.7 us
  Pallas kernels  50.1 us (98%)
  between operations  0.65 us (1%)
    pallas_call x1, Pallas kernels, shards(): pl.pallas_call(partial(upward, dims, peers), out_shape=[pltpu.VMEM(*r) fo...  48.7 us
    pallas_call x1, Pallas kernels, shards(): pl.pallas_call(partial(finishing, nx, ny), out_shape=[jax.ShapeDtypeStruc...  1.39 us

profile of v3, /device:TPU:0, one launch (start us, length us, event | category | flops | bytes accessed | tf_op | source)
XLA Modules:
  0.0 50.7 jit_solution(3426490242343955984)
XLA Ops:
  0.6 48.7 %shard_map.201 = (f32[14,14,2,8,128]{4,3,2,1,0:T(8,128)S(1)}, f32[12,12,2,8,128]{4,3,2,1,0:T(8,128)S(1)}, f32[12,12,8,128]{3,2,1,0:T(8,128)S(1)}, f32[10,10,8,12...) custom-call(f32[8,8,2,8,128]{4,3,2,1,0:T(8,128)} %bitcast.14, ...), custom_call_target="tpu_custom_call" | custom-call | tf_op jit(solution)/shard_map/pallas_call | solution.py:873
  49.3 1.4 %shard_map.202 = (f32[8,8,2,8,128]{4,3,2,1,0:T(8,128)}, f32[4,4,2,8,128]{4,3,2,1,0:T(8,128)}, f32[2,2,2,8,128]{4,3,2,1,0:T(8,128)}, f32[1,1,2,8,128]{4,3,2,1,0:T(8,128)}) custom-call(f32[14,14,2,8,128]{4,3,2,1,0:T(8,128)S(1)} %get-tuple-element.19.refs_0_, f32[12,12,2,8,128]{4,3,2,1,0:T(8,128)S(1)} %get-tuple-element.20.refs_1_, ...), custom_call_target="tpu_custom_call" | custom-call | tf_op jit(solution)/shard_map/pallas_call | solution.py:890

commit v4 on v3

--- a/solution.py
+++ b/solution.py
@@ -657,7 +657,6 @@
             target[row, cells] = value.reshape(value.shape[:1] + target.shape[2:])
 
     diagonals(2)
-    side2 = spread(S[third], REACH), spread(D[third], REACH)
     diagonals(1)
     diagonals(0)
     nx, ny = dims[0]
@@ -674,6 +673,7 @@
     for row, column, whole, copies in last:
         wait(copies)
         handed += share(row, column, whole, partner)
+    side2 = spread(S[third], REACH), spread(D[third], REACH)
     wait(handed)
     smooth_last()
     prolong(2, range(dims[2][0]))

time: 50.9 us -> 50.6 us (level)
  no operation moved by 1% of the time
where the time goes in v4:
time: 50.6 us; the launch traced here: 50.4 us
  Pallas kernels  49.8 us (98%)
  between operations  0.65 us (1%)
    pallas_call x1, Pallas kernels, shards(): pl.pallas_call(partial(upward, dims, peers), out_shape=[pltpu.VMEM(*r) fo...  48.4 us
    pallas_call x1, Pallas kernels, shards(): pl.pallas_call(partial(finishing, nx, ny), out_shape=[jax.ShapeDtypeStruc...  1.39 us

profile of v4, /device:TPU:0, one launch (start us, length us, event | category | flops | bytes accessed | tf_op | source)
XLA Modules:
  0.0 50.4 jit_solution(1149276440340530991)
XLA Ops:
  0.6 48.4 %shard_map.201 = (f32[14,14,2,8,128]{4,3,2,1,0:T(8,128)S(1)}, f32[12,12,2,8,128]{4,3,2,1,0:T(8,128)S(1)}, f32[12,12,8,128]{3,2,1,0:T(8,128)S(1)}, f32[10,10,8,12...) custom-call(f32[8,8,2,8,128]{4,3,2,1,0:T(8,128)} %bitcast.14, ...), custom_call_target="tpu_custom_call" | custom-call | tf_op jit(solution)/shard_map/pallas_call | solution.py:873
  49.0 1.4 %shard_map.202 = (f32[8,8,2,8,128]{4,3,2,1,0:T(8,128)}, f32[4,4,2,8,128]{4,3,2,1,0:T(8,128)}, f32[2,2,2,8,128]{4,3,2,1,0:T(8,128)}, f32[1,1,2,8,128]{4,3,2,1,0:T(8,128)}) custom-call(f32[14,14,2,8,128]{4,3,2,1,0:T(8,128)S(1)} %get-tuple-element.19.refs_0_, f32[12,12,2,8,128]{4,3,2,1,0:T(8,128)S(1)} %get-tuple-element.20.refs_1_, ...), custom_call_target="tpu_custom_call" | custom-call | tf_op jit(solution)/shard_map/pallas_call | solution.py:890
